TPU v7x, 32 devices: a whole 2x2x4 slice. The times are simulated.
32 devices in a mesh: param: 16 (over z, y, x), sensor: 2 (over core).
Axes of the slice: x: 2, y: 2, z: 4, core: 2. Of those that a mesh axis runs over, the one named last changes fastest.
Arguments:
- data: float32 [16, 512, 420], P(None, ('sensor', 'param')), may hold values from -6 to 6
- spectra: float32 [2, 512, 64, 421], P(None, 'sensor', 'param'), may hold values from -2 to 2
Outputs:
- gradient: float32 [16, 64, 420], P(None, 'param')
- rms: float32 [16], replicated
All inputs are finite; a program needn't handle non-finite values.
Results may differ from a plain program's by a relative error of at most 0.0003.
Values sent between devices are 32-bit elements; how exact they have to be, the bound alone decides.
A program may use at most 128 MiB of HBM per device.

v0:
```python
import math
import jax
import jax.numpy as jnp
from jax import lax
from jax.sharding import PartitionSpec as P


def spectral_tables(steps):
    length = 2 * steps
    freqs = steps + 1
    times = lax.broadcasted_iota(jnp.int32, (steps, freqs), 0)
    bins = lax.broadcasted_iota(jnp.int32, (steps, freqs), 1)
    phase = 2.0 * math.pi / length * (times * bins % length).astype(jnp.float32)
    forward = jnp.concatenate([jnp.cos(phase), -jnp.sin(phase)], axis=1)
    weight = jnp.where((bins == 0) | (bins == steps), 1.0, 2.0) / length
    backward = jnp.concatenate([(weight * jnp.cos(phase)).T, (-weight * jnp.sin(phase)).T], axis=0)
    return (forward, backward)


def to_spectrum(series, forward):
    vectors, sensors, steps = series.shape
    flat = jnp.dot(
        series.reshape(vectors * sensors, steps),
        forward,
        precision=lax.Precision.HIGHEST,
        preferred_element_type=jnp.float32,
    )
    return flat.reshape(vectors, sensors, forward.shape[1])


def contract(kernel, spectrum):
    return jnp.einsum(
        "spf,rsf->rpf",
        kernel,
        spectrum,
        precision=lax.Precision.HIGHEST,
        preferred_element_type=jnp.float32,
    )


def body(data, spectra):
    steps = data.shape[2]
    freqs = steps + 1
    forward, backward = spectral_tables(steps)
    whole = to_spectrum(lax.all_gather(data, "param", axis=1, tiled=True), forward)
    real_part = whole[..., :freqs]
    imag_part = whole[..., freqs:]
    kernel_re = spectra[0]
    kernel_im = spectra[1]
    out_re = contract(kernel_re, real_part) + contract(kernel_im, imag_part)
    out_im = contract(kernel_re, imag_part) - contract(kernel_im, real_part)
    vectors, points = (out_re.shape[0], out_re.shape[1])
    stacked = jnp.concatenate([out_re, out_im], axis=2).reshape(vectors * points, 2 * freqs)
    partial_field = jnp.dot(
        stacked, backward, precision=lax.Precision.HIGHEST, preferred_element_type=jnp.float32
    ).reshape(vectors, points, steps)
    count = points * lax.axis_size("param") * steps
    share = lax.psum_scatter(partial_field, "sensor", scatter_dimension=0, tiled=True)
    squares = lax.psum(jnp.sum(share * share, axis=(1, 2)), "param")
    scale = jnp.sqrt(squares / count + 1e-06)
    normalized = share / scale[:, None, None]
    gradient, rms_all = (
        lax.all_gather(normalized, "sensor", axis=0, tiled=True),
        lax.all_gather(scale, "sensor", axis=0, tiled=True),
    )
    return (gradient, rms_all)


def solution(mesh):
    in_specs = (P(None, ("sensor", "param"), None), P(None, "sensor", "param", None))
    out_specs = (P(None, "param", None), P())
    return jax.shard_map(body, mesh=mesh, in_specs=in_specs, out_specs=out_specs, check_vma=False)
```

profile of v0, /device:TPU:0, one launch (start us, length us, event | category | flops | bytes accessed | tf_op | source)
XLA Modules:
  0.0 326.7 jit_solution(8645191133042081712)
XLA Ops:
  7.2 0.0 copy-start
  7.2 0.0 all-gather.2.cloned.1.call-start
  7.2 0.7 all-gather.2.cloned.1.call-update
  7.9 0.0 reduce-scatter.2.cloned.1.call-start
  8.0 4.5 %sine_negate_fusion = (f32[420,421]{1,0:T(8,128)}, f32[420,421]{1,0:T(8,128)}) fusion(), kind=kLoop, calls=%fused_computation.39 | loop fusion | flops 1768200 | bytes 1414560 | tf_op jit(solution)/shard_map/neg | solution.py:14
  12.5 4.6 %sine_multiply_fusion = (f32[421,420]{0,1:T(8,128)}, f32[421,420]{0,1:T(8,128)}) fusion(f32[421]{0:T(512)S(1)} %fusion.42, f32[421]{0:T(512)S(1)} %select_multiply_fusion), kind=kLoop, calls=%fused_computation.34 | loop fusion | flops 1945020 | bytes 1417928 | tf_op jit(solution)/shard_map/mul | solution.py:16
  17.0 0.0 copy-done
  17.0 1.5 fusion.73
  18.5 1.5 fusion.71
  20.0 1.5 fusion.75
  21.6 1.5 fusion.77
  23.1 102.6 %all-gather.2.cloned.1.call-done = f32[16,256,420]{2,1,0:T(8,128)} async-done(((f32[16,16,420]{2,1,0:T(8,128)}), f32[16,256,420]{2,1,0:T(8,128)}) %all-gather.2.cloned.1.call-update) | async-done | bytes 6881296 | tf_op jit(solution)/shard_map/all_gather | solution.py:45
  125.7 51.7 %fusion.20 = f32[842,4096]{1,0:T(8,128)} fusion(f32[4096,420]{1,0:T(8,128)} %bitcast.71, f32[420,421]{1,0:T(8,128)} %get-tuple-element.6, f32[420,421]{1,0:T(8,128)} %get-tuple-element.7), kind=kOutput, calls=%fused_computation.20 | convolution fusion | flops 17382467584 | bytes 22091168 | tf_op jit(solution)/shard_map/dot_general | solution.py:22
  177.4 0.0 copy-start.4
  177.4 16.8 %copy.9 = f32[106,8,16,256]{3,2,1,0:T(8,128)} copy(f32[106,8,16,256]{3,1,2,0:T(8,128)} %bitcast.70) | data formatting | bytes 27787264
  194.2 0.0 copy-done.4
  194.2 0.0 copy-start.3
  194.2 14.2 %fusion.2 = f32[421,16,4]{1,2,0:T(4,128)} fusion(f32[848,16,256]{2,1,0:T(8,128)} %bitcast.66, f32[256,4,421]{0,1,2:T(4,128)S(1)} %copy-done.4), kind=kOutput, calls=%fused_computation.2 | convolution fusion | flops 82771968 | bytes 15627520 | tf_op jit(solution)/shard_map/spf,rsf->rpf/dot_general | solution.py:32
  208.5 2.1 copy.5
  210.6 0.0 copy-done.3
  210.6 0.0 copy-start.2
  210.6 14.2 %fusion = f32[421,16,4]{1,2,0:T(4,128)} fusion(f32[848,16,256]{2,1,0:T(8,128)} %bitcast.67, f32[256,4,421]{0,1,2:T(4,128)S(1)} %copy-done.3), kind=kOutput, calls=%fused_computation | convolution fusion | flops 82771968 | bytes 15627520 | tf_op jit(solution)/shard_map/spf,rsf->rpf/dot_general | solution.py:32
  224.8 2.1 copy.6
  226.9 0.0 copy-done.2
  226.9 0.0 copy-start.1
  226.9 14.3 %fusion.4 = f32[421,16,4]{1,2,0:T(4,128)} fusion(f32[848,16,256]{2,1,0:T(8,128)} %bitcast.68, f32[256,4,421]{0,1,2:T(4,128)S(1)} %copy-done.2), kind=kOutput, calls=%fused_computation.4 | convolution fusion | flops 82771968 | bytes 15627520 | tf_op jit(solution)/shard_map/spf,rsf->rpf/dot_general | solution.py:32
  241.2 2.1 copy.7
  243.3 0.0 copy-done.1
  243.3 0.0 copy-start.5
  243.3 0.0 copy-start.6
  243.3 14.1 %fusion.6 = f32[421,16,4]{1,2,0:T(4,128)} fusion(f32[848,16,256]{2,1,0:T(8,128)} %bitcast.69, f32[256,4,421]{0,1,2:T(4,128)S(1)} %copy-done.1), kind=kOutput, calls=%fused_computation.6 | convolution fusion | flops 82771968 | bytes 15627520 | tf_op jit(solution)/shard_map/spf,rsf->rpf/dot_general | solution.py:32
  257.4 0.0 copy-start.7
  257.4 1.5 copy.8
  258.9 1.0 add_bitcast_fusion
  259.9 0.9 subtract_bitcast_fusion
  260.8 0.0 copy-done.5
  260.8 0.0 copy-done.6
  260.8 2.3 fusion.24
  263.1 0.0 reduce-scatter.2.cloned.1.call-update
  263.1 0.0 copy-done.7
  263.1 0.6 dynamic-slice
  263.7 5.8 %reduce-scatter.2.cloned.1.call-done = f32[8,4,420]{2,0,1:T(8,128)} async-done(((f32[16,4,420]{2,0,1:T(8,128)}), f32[8,4,420]{2,0,1:T(8,128)}) %reduce-scatter.2.cloned.1.call-update) | async-done | bytes 53776 | tf_op jit(solution)/shard_map/reduce_scatter | solution.py:58
  269.5 1.0 multiply_reduce_fusion
  271.1 41.9 %psum.7 = f32[8]{0:T(128)S(1)} all-reduce(f32[8]{0:T(128)S(1)} %multiply_reduce_fusion), channel_id=1, replica_groups=mesh['param'=16,'sensor'=2] {'param'}, use_global_device_ids=true, to_apply=%region_2.3 | all-reduce | flops 8 | bytes 64 | tf_op jit(solution)/shard_map/psum | solution.py:59
  313.0 0.1 fusion.45
  313.1 0.9 broadcast_divide_fusion
  314.0 1.9 all_gather.10
  315.9 0.7 copy.4
  316.7 2.9 all-reduce
  (3 shorter events, 0.0 us)
Async XLA Ops:
  7.2 9.9 %copy-start = (f32[2,256,4,421]{1,2,3,0:T(4,128)S(1)}, f32[2,256,4,421]{1,2,3,0:T(4,128)}, u32[]{:S(2)}) copy-start(f32[2,256,4,421]{1,2,3,0:T(4,128)} %param.3) | copy-start | bytes 10346500
  7.2 118.6 %all-gather.2.cloned.1.call-start = ((), (), s32[]{:S(2)}) async-start(), calls=%async_computation.1 | async-start | bytes 8912896 | tf_op jit(solution)/shard_map/all_gather | solution.py:45
  7.9 261.6 %reduce-scatter.2.cloned.1.call-start = ((), (), s32[]{:S(2)}) async-start(), calls=%async_computation.2 | async-start | bytes 196608 | tf_op jit(solution)/shard_map/reduce_scatter | solution.py:58
  177.4 16.8 %copy-start.4 = (f32[256,4,421]{0,1,2:T(4,128)S(1)}, f32[256,4,421]{0,1,2:T(4,128)}, u32[]{:S(2)}) copy-start(f32[256,4,421]{0,1,2:T(4,128)} %fusion.73) | copy-start | bytes 5173252
  194.2 16.3 %copy-start.3 = (f32[256,4,421]{0,1,2:T(4,128)S(1)}, f32[256,4,421]{0,1,2:T(4,128)}, u32[]{:S(2)}) copy-start(f32[256,4,421]{0,1,2:T(4,128)} %fusion.71) | copy-start | bytes 5173252
  210.6 16.3 %copy-start.2 = (f32[256,4,421]{0,1,2:T(4,128)S(1)}, f32[256,4,421]{0,1,2:T(4,128)}, u32[]{:S(2)}) copy-start(f32[256,4,421]{0,1,2:T(4,128)} %fusion.75) | copy-start | bytes 5173252
  226.9 16.4 %copy-start.1 = (f32[256,4,421]{0,1,2:T(4,128)S(1)}, f32[256,4,421]{0,1,2:T(4,128)}, u32[]{:S(2)}) copy-start(f32[256,4,421]{0,1,2:T(4,128)} %fusion.77) | copy-start | bytes 5173252
  243.3 17.5 %copy-start.5 = (f32[421,420]{0,1:T(8,128)S(1)}, f32[421,420]{0,1:T(8,128)}, u32[]{:S(2)}) copy-start(f32[421,420]{0,1:T(8,128)} %get-tuple-element.8) | copy-start | bytes 2121844
  243.3 17.5 %copy-start.6 = (f32[421,420]{0,1:T(8,128)S(1)}, f32[421,420]{0,1:T(8,128)}, u32[]{:S(2)}) copy-start(f32[421,420]{0,1:T(8,128)} %get-tuple-element.9) | copy-start | bytes 2121844
  257.4 5.7 %copy-start.7 = (u32[32]{0:T(128)S(1)}, u32[32]{0:T(128)}, u32[]{:S(2)}) copy-start(u32[32]{0:T(128)} %constant.35) | copy-start | bytes 388
Sparse Core Ops, SparseCore 0:
  10.8 114.9 all-gather.1
  263.2 6.2 reduce-scatter.1
where the time goes:
time: 330 us; the launch traced here: 327 us
  matrix products  111 us (34%)
  waiting for transfers between devices  109 us (33%)
  blocking collectives  46.8 us (14%)
  local copies, waits for them, and re-layouts  32 us (10%)
  between operations  15 us (5%)
  other arithmetic  13 us (4%)
    all_gather x1, waiting for transfers between devices, body(): lax.all_gather(data, 'param', axis=1, tiled=True)  103 us
    dot_general x4, matrix products, contract(): jnp.einsum('spf,rsf->rpf', kernel, spectrum, precision=lax.Precision.HIGH...  56.8 us
    dot_general x1, matrix products, to_spectrum(): jnp.dot(series.reshape(vectors * sensors, steps), forward, precision=lax....  51.7 us
    psum x1, blocking collectives, body(): squares = lax.psum(jnp.sum(share * share, axis=(1, 2)), 'param')  41.9 us
    unnamed x20, local copies, waits for them, and re-layouts  18.2 us
    dot_general x8, local copies, waits for them, and re-layouts, contract(): jnp.einsum('spf,rsf->rpf', kernel, spectrum, precision=lax.Precision.HIGH...  13.8 us
  transfers between devices with their start and end apart: 2, of which 2 were waited for; matrix products, arithmetic and copies ran while one was open for 5% of the time, Pallas kernels for 0%

commit v1 on v0

--- a/solution.py
+++ b/solution.py
@@ -3,6 +3,12 @@
 import jax.numpy as jnp
 from jax import lax
 from jax.sharding import PartitionSpec as P
+
+
+def all_parts(array, axis, dim):
+    terms = lax.all_gather(array, axis, axis=0, tiled=False)
+    out = jnp.concatenate(terms, axis=dim)
+    return out
 
 
 def spectral_tables(steps):
@@ -42,7 +48,7 @@
     steps = data.shape[2]
     freqs = steps + 1
     forward, backward = spectral_tables(steps)
-    whole = to_spectrum(lax.all_gather(data, "param", axis=1, tiled=True), forward)
+    whole = to_spectrum(all_parts(data, "param", 1), forward)
     real_part = whole[..., :freqs]
     imag_part = whole[..., freqs:]
     kernel_re = spectra[0]

time: 330 us -> 313 us (0.948)
  matrix products: 111 us -> 97.3 us
    dot_general x4, matrix products: 56.8 us -> 45.5 us  [contract(): jnp.einsum('spf,rsf->rpf', kernel, spectrum, precision=lax.Precision.HIGH...]
    dot_general x8 -> x4, local copies, waits for them, and re-layouts: 13.8 us -> 6.04 us  [contract(): jnp.einsum('spf,rsf->rpf', kernel, spectrum, precision=lax.Precision.HIGH...]
    all_gather x0 -> x1, local copies, waits for them, and re-layouts: none -> 4.57 us  [all_parts(): terms = lax.all_gather(array, axis, axis=0, tiled=False)]
    unnamed x20 -> x26, local copies, waits for them, and re-layouts: 18.2 us -> 18.2 us
where the time goes in v1:
time: 313 us; the launch traced here: 309 us
  waiting for transfers between devices  109 us (35%)
  matrix products  97.3 us (31%)
  blocking collectives  46.8 us (15%)
  local copies, waits for them, and re-layouts  30.1 us (10%)
  between operations  15.1 us (5%)
  other arithmetic  11 us (4%)
    all_gather x1, waiting for transfers between devices, all_parts(): terms = lax.all_gather(array, axis, axis=0, tiled=False)  103 us
    dot_general x1, matrix products, to_spectrum(): jnp.dot(series.reshape(vectors * sensors, steps), forward, precision=lax....  49.6 us
    dot_general x4, matrix products, contract(): jnp.einsum('spf,rsf->rpf', kernel, spectrum, precision=lax.Precision.HIGH...  45.5 us
    psum x1, blocking collectives, body(): squares = lax.psum(jnp.sum(share * share, axis=(1, 2)), 'param')  41.9 us
    unnamed x26, local copies, waits for them, and re-layouts  18.2 us
  transfers between devices with their start and end apart: 2, of which 2 were waited for; matrix products, arithmetic and copies ran while one was open for 5% of the time, Pallas kernels for 0%

profile of v1, /device:TPU:0, one launch (start us, length us, event | category | flops | bytes accessed | tf_op | source)
XLA Modules:
  0.0 309.1 jit_solution(1585148342669971536)
XLA Ops:
  7.2 0.0 copy-start
  7.2 0.0 all-gather.3.cloned.1.call-start
  7.2 0.7 all-gather.3.cloned.1.call-update
  7.9 0.0 reduce-scatter.2.cloned.1.call-start
  8.0 4.5 %sine_negate_fusion = (f32[420,421]{1,0:T(8,128)}, f32[420,421]{1,0:T(8,128)}) fusion(), kind=kLoop, calls=%fused_computation.43 | loop fusion | flops 1768200 | bytes 1414560 | tf_op jit(solution)/shard_map/neg | solution.py:20
  12.5 4.5 %sine_multiply_fusion = (f32[421,420]{0,1:T(8,128)}, f32[421,420]{0,1:T(8,128)}) fusion(f32[421]{0:T(512)S(1)} %fusion.62, f32[421]{0:T(512)S(1)} %select_multiply_fusion), kind=kLoop, calls=%fused_computation.38 | loop fusion | flops 1945020 | bytes 1417928 | tf_op jit(solution)/shard_map/mul | solution.py:22
  17.0 0.0 copy-done
  17.0 1.5 fusion.91
  18.5 1.5 fusion.97
  20.0 1.5 fusion.93
  21.5 1.5 fusion.95
  23.1 102.7 %all-gather.3.cloned.1.call-done = f32[256,16,420]{2,1,0:T(8,128)} async-done(((f32[16,16,420]{2,1,0:T(8,128)}), f32[256,16,420]{2,1,0:T(8,128)}) %all-gather.3.cloned.1.call-update) | async-done | bytes 6881296 | tf_op jit(solution)/shard_map/all_gather | solution.py:9
  125.8 0.0 copy-start.7
  125.8 0.0 copy-start.8
  125.8 4.6 %copy.10 = f32[16,16,16,420]{3,2,0,1:T(8,128)S(1)} copy(f32[16,16,16,420]{3,2,1,0:T(8,128)} %bitcast.95) | data formatting | bytes 13762560 | tf_op jit(solution)/shard_map/all_gather | solution.py:9
  130.4 0.0 copy-done.7
  130.4 0.0 copy-done.8
  130.4 49.6 %fusion.20 = f32[842,4096]{1,0:T(8,128)} fusion(f32[4096,420]{1,0:T(8,128)S(1)} %bitcast.94, f32[420,421]{1,0:T(8,128)S(1)} %copy-done.7, f32[420,421]{1,0:T(8,128)S(1)} %copy-done.8), kind=kOutput, calls=%fused_computation.20 | convolution fusion | flops 17382467584 | bytes 22091168 | tf_op jit(solution)/shard_map/dot_general | solution.py:28
  180.0 0.0 copy-start.4
  180.0 16.8 %copy.14 = f32[106,8,16,256]{3,2,1,0:T(8,128)} copy(f32[106,8,16,256]{3,1,2,0:T(8,128)} %bitcast.93) | data formatting | bytes 27787264
  196.8 0.0 copy-done.4
  196.8 0.0 copy-start.3
  196.8 13.3 %fusion = f32[421,16,4]{1,2,0:T(4,128)S(1)} fusion(f32[848,16,256]{2,1,0:T(8,128)} %bitcast.89, f32[256,4,421]{0,1,2:T(4,128)S(1)} %copy-done.4), kind=kOutput, calls=%fused_computation | convolution fusion | flops 82771968 | bytes 15627520 | tf_op jit(solution)/shard_map/spf,rsf->rpf/dot_general | solution.py:38
  210.1 0.0 copy-done.3
  210.1 0.0 copy-start.2
  210.1 9.5 %fusion.42 = f32[16,4,421]{0,1,2:T(4,128)S(1)} fusion(f32[421,16,4]{1,2,0:T(4,128)S(1)} %fusion, f32[848,16,256]{2,1,0:T(8,128)} %bitcast.90, f32[256,4,421]{0,1,2:T(4,128)S(1)} %copy-done.3), kind=kOutput, calls=%fused_computation.31 | convolution fusion | flops 82798912 | bytes 15735296 | tf_op jit(solution)/shard_map/spf,rsf->rpf/dot_general | solution.py:38
  219.6 1.0 copy.11
  220.6 0.0 copy-done.2
  220.6 0.0 copy-start.1
  220.6 13.3 %fusion.4 = f32[421,16,4]{1,2,0:T(4,128)S(1)} fusion(f32[848,16,256]{2,1,0:T(8,128)} %bitcast.91, f32[256,4,421]{0,1,2:T(4,128)S(1)} %copy-done.2), kind=kOutput, calls=%fused_computation.4 | convolution fusion | flops 82771968 | bytes 15627520 | tf_op jit(solution)/shard_map/spf,rsf->rpf/dot_general | solution.py:38
  233.9 0.0 copy-done.1
  233.9 0.0 copy-start.5
  233.9 0.0 copy-start.6
  233.9 0.0 copy-start.9
  234.0 0.0 copy-start.10
  234.0 9.4 %fusion.32 = f32[16,4,421]{0,1,2:T(4,128)S(1)} fusion(f32[421,16,4]{1,2,0:T(4,128)S(1)} %fusion.4, f32[848,16,256]{2,1,0:T(8,128)} %bitcast.92, f32[256,4,421]{0,1,2:T(4,128)S(1)} %copy-done.1), kind=kOutput, calls=%fused_computation.29 | convolution fusion | flops 82798912 | bytes 15735296 | tf_op jit(solution)/shard_map/spf,rsf->rpf/dot_general | solution.py:38
  243.4 0.3 copy.12
  243.7 0.0 copy-done.5
  243.7 0.0 copy-done.6
  243.7 0.0 copy-done.9
  243.7 2.3 fusion.24
  246.0 0.0 reduce-scatter.2.cloned.1.call-update
  246.0 0.0 copy-done.10
  246.0 0.6 dynamic-slice
  246.6 5.3 %reduce-scatter.2.cloned.1.call-done = f32[8,4,420]{2,0,1:T(8,128)} async-done(((f32[16,4,420]{2,0,1:T(8,128)}), f32[8,4,420]{2,0,1:T(8,128)}) %reduce-scatter.2.cloned.1.call-update) | async-done | bytes 53776 | tf_op jit(solution)/shard_map/reduce_scatter | solution.py:64
  251.9 1.0 multiply_reduce_fusion
  253.6 41.9 %psum.7 = f32[8]{0:T(128)S(1)} all-reduce(f32[8]{0:T(128)S(1)} %multiply_reduce_fusion), channel_id=1, replica_groups=mesh['param'=16,'sensor'=2] {'param'}, use_global_device_ids=true, to_apply=%region_2.3 | all-reduce | flops 8 | bytes 64 | tf_op jit(solution)/shard_map/psum | solution.py:65
  295.5 0.1 fusion.65
  295.6 0.9 broadcast_divide_fusion
  296.5 1.9 all_gather.14
  298.4 0.7 copy.13
  299.1 2.9 all-reduce
  (3 shorter events, 0.0 us)
Async XLA Ops:
  7.2 9.9 %copy-start = (f32[2,256,4,421]{1,2,3,0:T(4,128)S(1)}, f32[2,256,4,421]{1,2,3,0:T(4,128)}, u32[]{:S(2)}) copy-start(f32[2,256,4,421]{1,2,3,0:T(4,128)} %param.3) | copy-start | bytes 10346500
  7.2 118.6 %all-gather.3.cloned.1.call-start = ((), (), s32[]{:S(2)}) async-start(), calls=%async_computation.2 | async-start | bytes 8912896 | tf_op jit(solution)/shard_map/all_gather | solution.py:9
  7.9 244.0 %reduce-scatter.2.cloned.1.call-start = ((), (), s32[]{:S(2)}) async-start(), calls=%async_computation.1 | async-start | bytes 196608 | tf_op jit(solution)/shard_map/reduce_scatter | solution.py:64
  125.8 4.6 %copy-start.7 = (f32[420,421]{1,0:T(8,128)S(1)}, f32[420,421]{1,0:T(8,128)}, u32[]{:S(2)}) copy-start(f32[420,421]{1,0:T(8,128)} %get-tuple-element.12) | copy-start | bytes 2121844
  125.8 4.6 %copy-start.8 = (f32[420,421]{1,0:T(8,128)S(1)}, f32[420,421]{1,0:T(8,128)}, u32[]{:S(2)}) copy-start(f32[420,421]{1,0:T(8,128)} %get-tuple-element.13) | copy-start | bytes 2121844
  180.0 16.8 %copy-start.4 = (f32[256,4,421]{0,1,2:T(4,128)S(1)}, f32[256,4,421]{0,1,2:T(4,128)}, u32[]{:S(2)}) copy-start(f32[256,4,421]{0,1,2:T(4,128)} %fusion.91) | copy-start | bytes 5173252
  196.8 13.3 %copy-start.3 = (f32[256,4,421]{0,1,2:T(4,128)S(1)}, f32[256,4,421]{0,1,2:T(4,128)}, u32[]{:S(2)}) copy-start(f32[256,4,421]{0,1,2:T(4,128)} %fusion.97) | copy-start | bytes 5173252
  210.1 10.5 %copy-start.2 = (f32[256,4,421]{0,1,2:T(4,128)S(1)}, f32[256,4,421]{0,1,2:T(4,128)}, u32[]{:S(2)}) copy-start(f32[256,4,421]{0,1,2:T(4,128)} %fusion.93) | copy-start | bytes 5173252
  220.6 13.3 %copy-start.1 = (f32[256,4,421]{0,1,2:T(4,128)S(1)}, f32[256,4,421]{0,1,2:T(4,128)}, u32[]{:S(2)}) copy-start(f32[256,4,421]{0,1,2:T(4,128)} %fusion.95) | copy-start | bytes 5173252
  233.9 9.8 %copy-start.5 = (f32[421,420]{0,1:T(8,128)S(1)}, f32[421,420]{0,1:T(8,128)}, u32[]{:S(2)}) copy-start(f32[421,420]{0,1:T(8,128)} %get-tuple-element.14) | copy-start | bytes 2121844
  233.9 9.8 %copy-start.6 = (f32[421,420]{0,1:T(8,128)S(1)}, f32[421,420]{0,1:T(8,128)}, u32[]{:S(2)}) copy-start(f32[421,420]{0,1:T(8,128)} %get-tuple-element.15) | copy-start | bytes 2121844
  233.9 9.8 %copy-start.9 = (f32[16,4,421]{2,0,1:T(8,128)S(1)}, f32[16,4,421]{2,0,1:T(8,128)}, u32[]{:S(2)}) copy-start(f32[16,4,421]{2,0,1:T(8,128)} %copy.11) | copy-start | bytes 323332
  234.0 12.1 %copy-start.10 = (u32[32]{0:T(128)S(1)}, u32[32]{0:T(128)}, u32[]{:S(2)}) copy-start(u32[32]{0:T(128)} %constant.35) | copy-start | bytes 388
Sparse Core Ops, SparseCore 0:
  10.8 115.0 all-gather.2
  246.2 5.7 reduce-scatter.1
